TPU v7x, 256 devices: a whole 4x4x8 slice. The times are simulated.
256 devices in a mesh: cluster: 8 (over z), member: 32 (over y, x, core).
Axes of the slice: x: 4, y: 4, z: 8, core: 2. Of those that a mesh axis runs over, the one named last changes fastest.
Arguments:
- factors: float32 [512, 1024, 1024], P(('cluster', 'member')), as said below
- panels: float32 [512, 1024, 256], P(('cluster', 'member')), may hold values from -0.046875 to 0.046875
- sizes: int32 [512], P(('cluster', 'member')), may hold values from 512 to 1024
- glue_index: int32 [512, 256], P(('cluster', 'member')), may hold values from 0 to 1023, as said below
- loads: float32 [8192, 256], P(('cluster', 'member')), may hold values from -6 to 6
Outputs:
- dual_rows: float32 [8192, 1024], P(('cluster', 'member'))
- products: float32 [8192, 256], P(('cluster', 'member'))
Inputs may be any that keep to these rules, and one draw needn't show every extreme that they name: `glue_index`: the 256 entries of one subdomain are distinct; at most 16 of them lie in any one aligned block of 1024 // 32 dual rows, and every subdomain has 16 in some block. `factors`: strictly upper entries are zero; diagonal entries positive.
All inputs are finite; a program needn't handle non-finite values.
Results may differ from a plain program's by a relative error of at most 0.0003.
Values sent between devices are 32-bit elements; how exact they have to be, the bound alone decides.
A program may use at most 192 MiB of HBM per device.

v0:
```python
import math

import jax
import jax.numpy as jnp
from jax import lax
from jax.sharding import PartitionSpec as P

BLOCK = 128
NDUAL = 1024
IFACE = 8


PRECISE = lax.Precision.HIGHEST


def side_by_side(arrays, axis, split_dim, concat_dim, along):
    widths = [math.prod(a.shape[along:]) for a in arrays]
    both = jnp.concatenate(
        [a.reshape(*a.shape[:along], w) for a, w in zip(arrays, widths)], axis=along
    )
    out = lax.all_to_all(both, axis, split_axis=split_dim, concat_axis=concat_dim, tiled=True)
    pieces = jnp.split(out, [sum(widths[:k]) for k in range(1, len(widths))], axis=along)
    return tuple((b.reshape(*out.shape[:along], *a.shape[along:]) for a, b in zip(arrays, pieces)))


def sent_to_all(value, axis):
    copies = jnp.broadcast_to(value, (lax.axis_size(axis), *value.shape))
    return lax.all_to_all(copies, axis, split_axis=0, concat_axis=0, tiled=True)


def joined_along(pieces, dim):
    lengths = list(pieces.shape[1:])
    lengths[dim] *= pieces.shape[0]
    return jnp.moveaxis(pieces, 0, dim).reshape(lengths)


def gather_directly(value, axis, dim):
    pieces = sent_to_all(value, axis)
    return joined_along(pieces, dim)


def extended(value, sides, width):
    for axis, dim in sides:
        peers, length = (lax.axis_size(axis), value.shape[dim])
        up = [(i, (i + 1) % peers) for i in range(peers)]
        down = [(j, i) for i, j in up]
        last = lax.slice_in_dim(value, length - width, length, axis=dim)
        leading = lax.slice_in_dim(value, 0, width, axis=dim)
        before = lax.ppermute(last, axis, up)
        after = lax.ppermute(leading, axis, down)
        value = jnp.concatenate([before, value, after], axis=dim)
    return value


def inner_rows(left_side, right_side):
    return lax.dot_general(
        left_side,
        right_side,
        (((0,), (0,)), ((), ())),
        precision=PRECISE,
        preferred_element_type=jnp.float32,
    )


def live_lower(factor, live_size, first_row, row_count):
    full_rows = lax.dynamic_slice_in_dim(factor, first_row, row_count, 0)
    row_ids = first_row + lax.broadcasted_iota(jnp.int32, full_rows.shape, 0)
    col_ids = lax.broadcasted_iota(jnp.int32, full_rows.shape, 1)
    keeping = (row_ids < live_size) & (col_ids < live_size) & (col_ids <= row_ids)
    return jnp.where(keeping, full_rows, (row_ids == col_ids).astype(jnp.float32))


def solve_panel(factor, gluing, live_size):
    stride = BLOCK
    row_ids = lax.broadcasted_iota(jnp.int32, gluing.shape, 0)
    masked = jnp.where(row_ids < live_size, gluing, jnp.zeros_like(gluing))
    blocks = (live_size + stride - 1) // stride

    def advance(block_index, solved):
        first_row = block_index * stride
        band_rows = live_lower(factor, live_size, first_row, stride)
        remainder = lax.dynamic_slice_in_dim(masked, first_row, stride, 0) - jnp.dot(
            band_rows, solved, precision=PRECISE, preferred_element_type=jnp.float32
        )
        square = lax.dynamic_slice_in_dim(band_rows, first_row, stride, 1)
        solved_block = lax.linalg.triangular_solve(square, remainder, left_side=True, lower=True)
        return lax.dynamic_update_slice_in_dim(solved, solved_block, first_row, 0)

    return lax.fori_loop(0, blocks, advance, jnp.zeros_like(masked))


def on_device(factors, panels, sizes, glue_index, loads):
    dual_order = NDUAL
    members = lax.axis_size("member")
    row_share = loads.shape[0]
    sub_count = factors.shape[0]
    panel_width = glue_index.shape[1]
    columns = lax.broadcasted_iota(jnp.int32, (panel_width, dual_order), 1)
    local_duals = []
    for sub_slot in range(sub_count):
        solved = solve_panel(factors[sub_slot], panels[sub_slot], sizes[sub_slot])
        local_duals.append(inner_rows(solved, solved))
    capacity = 2 * panel_width // members
    slot_total = members * capacity
    slot_ids = lax.broadcasted_iota(jnp.int32, (slot_total, panel_width), 0)
    earlier = lax.broadcasted_iota(jnp.int32, (panel_width, panel_width), 1) < lax.broadcasted_iota(
        jnp.int32, (panel_width, panel_width), 0
    )
    value_list = []
    label_list = []
    for sub_slot in range(sub_count):
        glue = glue_index[sub_slot]
        owner = glue // row_share
        same_owner = (owner[:, None] == owner[None, :]) & earlier
        rank = jnp.sum(same_owner.astype(jnp.int32), axis=1)
        target = owner * capacity + rank
        dispatch = slot_ids == target[None, :]
        values = jnp.dot(
            dispatch.astype(jnp.float32),
            local_duals[sub_slot],
            precision=PRECISE,
            preferred_element_type=jnp.float32,
        )
        filled = jnp.sum(dispatch.astype(jnp.int32), axis=1)
        label_sum = jnp.sum(jnp.where(dispatch, (glue % row_share)[None, :], 0), axis=1)
        labels = jnp.where(filled > 0, label_sum, row_share)
        value_list.append(values.reshape(members, capacity, panel_width))
        label_list.append(labels.reshape(members, capacity))
    sent_values = jnp.concatenate(value_list, axis=1)
    sent_labels = jnp.concatenate(label_list, axis=1)
    sent_columns = jnp.broadcast_to(glue_index[None, :, :], (members, sub_count, panel_width))
    got_values, got_labels, got_columns = (
        lax.all_to_all(sent_values, "member", split_axis=0, concat_axis=0, tiled=True),
        *side_by_side((sent_labels, sent_columns), "member", 0, 0, 1),
    )
    owned_ids = lax.broadcasted_iota(jnp.int32, (row_share, capacity), 0)

    def place_source(summed, items):
        source_values, source_labels, source_columns = items
        for sub_slot in range(sub_count):
            block_values = source_values[sub_slot * capacity : (sub_slot + 1) * capacity]
            block_labels = source_labels[sub_slot * capacity : (sub_slot + 1) * capacity]
            column_map = (source_columns[sub_slot][:, None] == columns).astype(jnp.float32)
            spread = jnp.dot(
                block_values, column_map, precision=PRECISE, preferred_element_type=jnp.float32
            )
            row_map = (owned_ids == block_labels[None, :]).astype(jnp.float32)
            summed = summed + jnp.dot(
                row_map, spread, precision=PRECISE, preferred_element_type=jnp.float32
            )
        return (summed, None)

    dual_rows, unused = lax.scan(
        place_source,
        jnp.zeros((row_share, dual_order), jnp.float32),
        (got_values, got_labels, got_columns),
    )
    raw_rows = jnp.dot(
        dual_rows,
        gather_directly(loads, "member", 0),
        precision=PRECISE,
        preferred_element_type=jnp.float32,
    )
    width_iface = IFACE
    padded = extended(raw_rows, (("cluster", 0),), width_iface)
    previous_rows = padded[:width_iface]
    middle = padded[width_iface : width_iface + row_share]
    next_rows = padded[width_iface + row_share :]
    between = jnp.zeros((row_share - 2 * width_iface, raw_rows.shape[1]), jnp.float32)
    products = middle + jnp.concatenate([previous_rows, between, next_rows], axis=0)
    return (dual_rows, products)


def solution(mesh):
    return jax.shard_map(
        on_device,
        mesh=mesh,
        in_specs=(
            P(("cluster", "member"), None, None),
            P(("cluster", "member"), None, None),
            P(("cluster", "member")),
            P(("cluster", "member"), None),
            P(("cluster", "member"), None),
        ),
        out_specs=(P(("cluster", "member"), None), P(("cluster", "member"), None)),
        check_vma=False,
    )
```

profile of v0, /device:TPU:1, one launch (start us, length us, event | category | flops | bytes accessed | tf_op | source)
XLA Modules:
  0.0 338.0 jit_solution(7217481076179698997)
XLA Ops:
  0.6 0.8 and_select_fusion.2
  1.4 0.8 and_select_fusion
  2.4 0.7 and_select_fusion.1
  4.0 0.7 copy.8
  4.8 0.7 all_to_all.14
  5.5 8.6 %all-to-all-start = ((s32[32,1,544]{2,1,0:T(1,128)}), s32[32,1,544]{2,1,0:T(1,128)S(1)}, u32[]{:S(2)}, u32[]{:S(2)}) async-start(s32[32,1,544]{2,1,0:T(1,128)} %all_to_all.14), calls=%async_computation | async-start | bytes 163840 | tf_op jit(solution)/shard_map/all_to_all | solution.py:21
  14.1 1.3 fusion.23
  16.0 1.2 iota_compare_fusion.21
  17.8 8.5 %slice_bitcast_fusion.3 = (f32[1024,1024]{1,0:T(8,128)}, f32[1024,1024]{1,0:T(8,128)}) fusion(f32[2,1024,1024]{2,1,0:T(8,128)} %param.13), kind=kLoop, calls=%fused_computation.48 | loop fusion | bytes 16777216 | tf_op jit(solution)/shard_map/squeeze | solution.py:101
  26.3 1.6 bitcast_select_fusion.1
  28.0 70.7 %while.33 = (s32[]{:T(128)}, f32[1024,256]{1,0:T(8,128)S(1)}, s32[]{:T(128)}, s32[]{:T(128)}, f32[1024,1024]{1,0:T(8,128)}, /*index=5*/f32[1024,256]{1,0:T(8,128)}, s32[]{:T(128)}, s32[]{:T(128)}, s32[]{:T(128)}, s32[]{:T(128)}) while((s32[]{:T(128)}, f32[1024,256]{1,0:T(8,128)S(1)}, s32[]{:T(128)}, s32[]{:T(128)}, f32[1024,1024]{1,0:T(8,128)}, ...), condition=%wide.region_5.7_spmd, body=%wide.region_4.6_spmd.sunk | while | flops 453838208 | bytes 3345843 | solution.py:89
  29.2 1.3 convert_select_fusion.5
  30.5 9.8 %custom-call.10 = f32[1,128,128]{1,2,0:T(8,128)S(1)} custom-call(f32[1,128,128]{2,1,0:T(8,128)S(1)} %select_bitcast_fusion.5), custom_call_target="InvertDiagBlocksLowerTriangular" | custom-call | tf_op jit(solution)/shard_map/while/body/triangular_solve/custom-call.1 | solution.py:86
  40.3 1.5 convolution_subtract_fusion.5
  43.3 1.3 convert_select_fusion.5
  44.6 9.8 %custom-call.10 = f32[1,128,128]{1,2,0:T(8,128)S(1)} custom-call(f32[1,128,128]{2,1,0:T(8,128)S(1)} %select_bitcast_fusion.5), custom_call_target="InvertDiagBlocksLowerTriangular" | custom-call | tf_op jit(solution)/shard_map/while/body/triangular_solve/custom-call.1 | solution.py:86
  54.4 1.5 convolution_subtract_fusion.5
  57.5 1.3 convert_select_fusion.5
  58.7 9.8 %custom-call.10 = f32[1,128,128]{1,2,0:T(8,128)S(1)} custom-call(f32[1,128,128]{2,1,0:T(8,128)S(1)} %select_bitcast_fusion.5), custom_call_target="InvertDiagBlocksLowerTriangular" | custom-call | tf_op jit(solution)/shard_map/while/body/triangular_solve/custom-call.1 | solution.py:86
  68.6 1.5 convolution_subtract_fusion.5
  71.6 1.3 convert_select_fusion.5
  72.9 9.8 %custom-call.10 = f32[1,128,128]{1,2,0:T(8,128)S(1)} custom-call(f32[1,128,128]{2,1,0:T(8,128)S(1)} %select_bitcast_fusion.5), custom_call_target="InvertDiagBlocksLowerTriangular" | custom-call | tf_op jit(solution)/shard_map/while/body/triangular_solve/custom-call.1 | solution.py:86
  82.7 1.5 convolution_subtract_fusion.5
  85.8 1.3 convert_select_fusion.5
  87.0 9.8 %custom-call.10 = f32[1,128,128]{1,2,0:T(8,128)S(1)} custom-call(f32[1,128,128]{2,1,0:T(8,128)S(1)} %select_bitcast_fusion.5), custom_call_target="InvertDiagBlocksLowerTriangular" | custom-call | tf_op jit(solution)/shard_map/while/body/triangular_solve/custom-call.1 | solution.py:86
  96.9 1.5 convolution_subtract_fusion.5
  98.7 1.8 fusion.25
  101.1 107.2 %while.32 = (s32[]{:T(128)}, f32[1024,256]{1,0:T(8,128)S(1)}, s32[]{:T(128)}, s32[]{:T(128)}, f32[1024,1024]{1,0:T(8,128)}, /*index=5*/f32[1024,256]{1,0:T(8,128)S(1)}, s32[]{:T(128)}, s32[]{:T(128)}, s32[]{:T(128)}, s32[]{:T(128)}) while((s32[]{:T(128)}, f32[1024,256]{1,0:T(8,128)S(1)}, s32[]{:T(128)}, s32[]{:T(128)}, ...), condition=%wide.region_2.4_spmd, body=%wide.region_1.3_spmd.sunk | while | flops 453838208 | bytes 3345843 | solution.py:89
  102.4 1.3 convert_select_fusion.4
  103.7 9.8 %custom-call.9 = f32[1,128,128]{1,2,0:T(8,128)S(1)} custom-call(f32[1,128,128]{2,1,0:T(8,128)S(1)} %select_bitcast_fusion.4), custom_call_target="InvertDiagBlocksLowerTriangular" | custom-call | tf_op jit(solution)/shard_map/while/body/triangular_solve/custom-call.1 | solution.py:86
  113.5 0.6 convolution_subtract_fusion.4
  115.8 1.3 convert_select_fusion.4
  117.1 9.8 %custom-call.9 = f32[1,128,128]{1,2,0:T(8,128)S(1)} custom-call(f32[1,128,128]{2,1,0:T(8,128)S(1)} %select_bitcast_fusion.4), custom_call_target="InvertDiagBlocksLowerTriangular" | custom-call | tf_op jit(solution)/shard_map/while/body/triangular_solve/custom-call.1 | solution.py:86
  126.9 0.6 convolution_subtract_fusion.4
  129.2 1.3 convert_select_fusion.4
  130.5 9.8 %custom-call.9 = f32[1,128,128]{1,2,0:T(8,128)S(1)} custom-call(f32[1,128,128]{2,1,0:T(8,128)S(1)} %select_bitcast_fusion.4), custom_call_target="InvertDiagBlocksLowerTriangular" | custom-call | tf_op jit(solution)/shard_map/while/body/triangular_solve/custom-call.1 | solution.py:86
  140.3 0.6 convolution_subtract_fusion.4
  142.5 1.3 convert_select_fusion.4
  143.8 9.8 %custom-call.9 = f32[1,128,128]{1,2,0:T(8,128)S(1)} custom-call(f32[1,128,128]{2,1,0:T(8,128)S(1)} %select_bitcast_fusion.4), custom_call_target="InvertDiagBlocksLowerTriangular" | custom-call | tf_op jit(solution)/shard_map/while/body/triangular_solve/custom-call.1 | solution.py:86
  153.6 0.6 convolution_subtract_fusion.4
  154.6 0.6 broadcast_compare_fusion.4
  155.9 1.3 convert_select_fusion.4
  157.2 9.8 %custom-call.9 = f32[1,128,128]{1,2,0:T(8,128)S(1)} custom-call(f32[1,128,128]{2,1,0:T(8,128)S(1)} %select_bitcast_fusion.4), custom_call_target="InvertDiagBlocksLowerTriangular" | custom-call | tf_op jit(solution)/shard_map/while/body/triangular_solve/custom-call.1 | solution.py:86
  167.0 0.6 convolution_subtract_fusion.4
  168.0 0.6 broadcast_compare_fusion.4
  169.3 1.3 convert_select_fusion.4
  170.6 9.8 %custom-call.9 = f32[1,128,128]{1,2,0:T(8,128)S(1)} custom-call(f32[1,128,128]{2,1,0:T(8,128)S(1)} %select_bitcast_fusion.4), custom_call_target="InvertDiagBlocksLowerTriangular" | custom-call | tf_op jit(solution)/shard_map/while/body/triangular_solve/custom-call.1 | solution.py:86
  180.4 0.6 convolution_subtract_fusion.4
  182.7 1.3 convert_select_fusion.4
  184.0 9.8 %custom-call.9 = f32[1,128,128]{1,2,0:T(8,128)S(1)} custom-call(f32[1,128,128]{2,1,0:T(8,128)S(1)} %select_bitcast_fusion.4), custom_call_target="InvertDiagBlocksLowerTriangular" | custom-call | tf_op jit(solution)/shard_map/while/body/triangular_solve/custom-call.1 | solution.py:86
  193.8 0.6 convolution_subtract_fusion.4
  196.0 1.3 convert_select_fusion.4
  197.3 9.8 %custom-call.9 = f32[1,128,128]{1,2,0:T(8,128)S(1)} custom-call(f32[1,128,128]{2,1,0:T(8,128)S(1)} %select_bitcast_fusion.4), custom_call_target="InvertDiagBlocksLowerTriangular" | custom-call | tf_op jit(solution)/shard_map/while/body/triangular_solve/custom-call.1 | solution.py:86
  207.1 0.6 convolution_subtract_fusion.4
  208.3 1.8 fusion.24
  210.6 1.1 pad_maximum_fusion
  211.7 49.5 %all-to-all-start.1 = ((f32[32,32,256]{2,1,0:T(8,128)}), f32[32,32,256]{2,1,0:T(8,128)S(1)}, u32[]{:S(2)}, u32[]{:S(2)}) async-start(f32[32,32,256]{2,1,0:T(8,128)} %pad_maximum_fusion), calls=%async_computation.1 | async-start | bytes 2097152 | tf_op jit(solution)/shard_map/all_to_all | solution.py:133
  261.4 16.9 %all-to-all-done.1 = f32[32,32,256]{2,1,0:T(8,128)S(1)} async-done(((f32[32,32,256]{2,1,0:T(8,128)}), f32[32,32,256]{2,1,0:T(8,128)S(1)}, u32[]{:S(2)}, u32[]{:S(2)}) %all-to-all-start.1) | async-done | bytes 1048608 | tf_op jit(solution)/shard_map/all_to_all | solution.py:133
  278.3 1.1 broadcast_in_dim.63
  279.3 4.0 %all-to-all-start.2 = ((f32[32,32,256]{2,1,0:T(8,128)}), f32[32,32,256]{2,1,0:T(8,128)S(1)}, u32[]{:S(2)}, u32[]{:S(2)}) async-start(f32[32,32,256]{2,1,0:T(8,128)} %broadcast_in_dim.63), calls=%async_computation.2 | async-start | bytes 2097152 | tf_op jit(solution)/shard_map/all_to_all | solution.py:28
  283.3 49.0 %while.34 = (s32[]{:T(128)}, f32[32,1024]{1,0:T(8,128)S(1)}, s32[32,32]{1,0:T(8,128)S(1)}, f32[32,32,256]{2,1,0:T(8,128)S(1)}, s32[32,2,256]{2,1,0:T(2,128)S(1)}, /*index=5*/s32[]{:T(128)}, s32[]{:T(128)}, s32[]{}, s32[]{}) while((s32[]{:T(128)}, f32[32,1024]{1,0:T(8,128)S(1)}, s32[32,32]{1,0:T(8,128)S(1)}, ...), condition=%wide.region_11.13_spmd.clone.clone, body=%wide.region_10.12_spmd.clone.clone.sunk | while | flops 113869824 | bytes 826135 | solution.py:153
  333.1 3.3 collective-permute-start.1
  336.4 0.9 collective-permute-done
  337.3 0.7 maximum_add_fusion
  (323 shorter events, 69.4 us)
Async XLA Ops:
  5.5 206.1 %all-to-all-start = ((s32[32,1,544]{2,1,0:T(1,128)}), s32[32,1,544]{2,1,0:T(1,128)S(1)}, u32[]{:S(2)}, u32[]{:S(2)}) async-start(s32[32,1,544]{2,1,0:T(1,128)} %all_to_all.14), calls=%async_computation | async-start | bytes 163840 | tf_op jit(solution)/shard_map/all_to_all | solution.py:21
  17.8 8.5 %copy-start.1 = (f32[2,1024,256]{2,1,0:T(8,128)S(1)}, f32[2,1024,256]{2,1,0:T(8,128)}, u32[]{:S(2)}) copy-start(f32[2,1024,256]{2,1,0:T(8,128)} %param.14) | copy-start | bytes 6291460
  208.3 69.9 %copy-start.2 = (f32[32,256]{1,0:T(8,128)S(1)}, f32[32,256]{1,0:T(8,128)}, u32[]{:S(2)}) copy-start(f32[32,256]{1,0:T(8,128)} %param.17) | copy-start | bytes 98308
  211.7 66.6 %all-to-all-start.1 = ((f32[32,32,256]{2,1,0:T(8,128)}), f32[32,32,256]{2,1,0:T(8,128)S(1)}, u32[]{:S(2)}, u32[]{:S(2)}) async-start(f32[32,32,256]{2,1,0:T(8,128)} %pad_maximum_fusion), calls=%async_computation.1 | async-start | bytes 2097152 | tf_op jit(solution)/shard_map/all_to_all | solution.py:133
  279.3 53.0 %all-to-all-start.2 = ((f32[32,32,256]{2,1,0:T(8,128)}), f32[32,32,256]{2,1,0:T(8,128)S(1)}, u32[]{:S(2)}, u32[]{:S(2)}) async-start(f32[32,32,256]{2,1,0:T(8,128)} %broadcast_in_dim.63), calls=%async_computation.2 | async-start | bytes 2097152 | tf_op jit(solution)/shard_map/all_to_all | solution.py:28
  332.4 5.6 %copy-start = (f32[32,1024]{1,0:T(8,128)}, f32[32,1024]{1,0:T(8,128)S(1)}, u32[]{:S(2)}) copy-start(f32[32,1024]{1,0:T(8,128)S(1)} %get-tuple-element.110) | copy-start | bytes 393220
  333.0 4.3 %collective-permute-start = (f32[8,256]{1,0:T(8,128)S(1)}, f32[8,256]{1,0:T(8,128)S(1)}, u32[]{:S(2)}, u32[]{:S(2)}) collective-permute-start(f32[8,256]{1,0:T(8,128)S(1)} %get-tuple-element.208), channel_id=1, source_target_pairs={{0,32},{32,64},{64,96},{96,128},{128,160},{160,192},{192,224},{224... | collective-permute-start | bytes 24584 | tf_op jit(solution)/shard_map/ppermute | solution.py:49
  333.1 4.2 %collective-permute-start.1 = (f32[8,256]{1,0:T(8,128)S(1)}, f32[8,256]{1,0:T(8,128)S(1)}, u32[]{:S(2)}, u32[]{:S(2)}) collective-permute-start(f32[8,256]{1,0:T(8,128)S(1)} %get-tuple-element.209), channel_id=1, source_target_pairs={{32,0},{64,32},{96,64},{128,96},{160,128},{192,160},{224,192},{0,2... | collective-permute-start | bytes 24584 | tf_op jit(solution)/shard_map/ppermute | solution.py:50
where the time goes:
time: 342 us; the launch traced here: 338 us
  other arithmetic  168 us (49%)
  matrix products  66.6 us (19%)
  starting transfers between devices  65.4 us (19%)
  waiting for transfers between devices  17.8 us (5%)
  local copies, waits for them, and re-layouts  15.8 us (5%)
    another operation x26, other arithmetic, advance(): lax.linalg.triangular_solve(square, remainder, left_side=True, lower=True)  128 us
    all_to_all x1, starting transfers between devices, on_device(): lax.all_to_all(sent_values, 'member', split_axis=0, concat_axis=0, tiled=...  49.5 us
    dot_general x64, matrix products, place_source(): jnp.dot(block_values, column_map, precision=PRECISE, preferred_element_ty...  32 us
    all_to_all x1, waiting for transfers between devices, on_device(): lax.all_to_all(sent_values, 'member', split_axis=0, concat_axis=0, tiled=...  16.9 us
    select_n x13, other arithmetic, live_lower(): jnp.where(keeping, full_rows, (row_ids == col_ids).astype(jnp.float32))  16.3 us
    dot_general x13, matrix products, advance(): jnp.dot(band_rows, solved, precision=PRECISE, preferred_element_type=jnp....  12.9 us
    dot_general x64, matrix products, place_source(): jnp.dot(row_map, spread, precision=PRECISE, preferred_element_type=jnp.fl...  12.6 us
    all_to_all x1, starting transfers between devices, side_by_side(): lax.all_to_all(both, axis, split_axis=split_dim, concat_axis=concat_dim,...  8.58 us
  transfers between devices with their start and end apart: 5, of which 2 were waited for; matrix products, arithmetic and copies ran while one was open for 72% of the time, Pallas kernels for 0%

commit v1 on v0

v1 whole, which is shorter than its diff:
```python
import functools

import jax
import jax.numpy as jnp
from jax import lax
from jax.experimental import pallas as pl
from jax.experimental.pallas import tpu as pltpu
from jax.sharding import PartitionSpec as P

ORDER = 1024
PANEL = 256
NDUAL = 1024
MEMBERS = 32
CLUSTERS = 8
SHARE = NDUAL // MEMBERS
CAP = 2 * PANEL // MEMBERS
SUBS = 2
IFACE = 8
LANES = 128
STEP = 128
STEPS = ORDER // STEP
BASE = 32
TILES = NDUAL // LANES
F32, BF16, I32 = jnp.float32, jnp.bfloat16, jnp.int32
MESH = pl.DeviceIdType.MESH


def iota(shape, dim):
    return lax.broadcasted_iota(I32, shape, dim)


def split(x):
    high = x.astype(BF16)
    return high, (x - high.astype(F32)).astype(BF16)


def dot(a, b, dims=((1,), (0,))):
    return lax.dot_general(a, b, (dims, ((), ())), preferred_element_type=F32)


def dot3(a, b):
    a_high, a_low = a
    b_high, b_low = b
    left = jnp.concatenate([a_high, a_low], axis=1)
    right = jnp.concatenate([b_high, b_high], axis=0)
    return dot(left, right) + dot(a_high, b_low)


def lanes_from(x, index):
    return jnp.take_along_axis(x, index, axis=1, mode="promise_in_bounds")


def base_inverses(block):
    group = iota((BASE, LANES), 1) // BASE
    packed = jnp.zeros((BASE, LANES), F32)
    for q in range(LANES // BASE):
        packed = jnp.where(group == q, block[q * BASE : (q + 1) * BASE], packed)
    count = BASE // 8
    lane = iota((8, LANES), 1)
    first = (lane // BASE) * BASE
    unit, within, start, scale = [], lane % BASE, [], jnp.zeros((1, LANES), F32)
    for v in range(count):
        rows = packed[v * 8 : (v + 1) * 8]
        row_id = iota((8, LANES), 0) + v * 8
        inverse = 1.0 / lanes_from(rows, first + row_id)
        unit.append(jnp.where(within < row_id, rows * inverse, 0.0))
        start.append(jnp.where(within == row_id, 1.0, 0.0))
        scale = scale + jnp.sum(jnp.where(within == row_id, inverse, 0.0), axis=0, keepdims=True)
    result = start
    for j in range(BASE - 1):
        row = jnp.broadcast_to(result[j // 8][j % 8 : j % 8 + 1], (8, LANES))
        for v in range((j + 1) // 8, count):
            result[v] = result[v] - lanes_from(unit[v], first + j) * row
    scaled = jnp.concatenate(result, axis=0) * scale
    return jnp.concatenate(
        [jnp.where(group == q, scaled, 0.0) for q in range(LANES // BASE)], axis=0
    )


def block_inverse(block):
    inverse = base_inverses(block)
    size = BASE
    while size < STEP:
        row, col = iota(block.shape, 0) // size, iota(block.shape, 1) // size
        below = split(jnp.where((row % 2 == 1) & (col == row - 1), block, 0.0))
        picked = [
            inverse[k * size : (k + 1) * size] for k in range(1, STEP // size, 2)
        ]
        lower = jnp.concatenate(picked, axis=0)
        change = dot3(split(dot3(split(lower), below)), split(inverse))
        pieces = []
        for k in range(STEP // size):
            piece = inverse[k * size : (k + 1) * size]
            if k % 2:
                piece = piece - change[(k // 2) * size : (k // 2 + 1) * size]
            pieces.append(piece)
        inverse = jnp.concatenate(pieces, axis=0)
        size *= 2
    return inverse


def kernel(
    sizes, factors, panels, glue, loads, dual_out, products_out,
    factor, rhs, solved_high, solved_low, diag_high, diag_low, dispatch,
    outgoing, incoming, columns, rank_rows, ranks, all_loads,
    spread_high, spread_low, placing, stacked, raw, before, after,
    factor_sem, panel_sem, value_send, value_recv, column_send, column_recv,
    rank_send, rank_recv, load_send, load_recv, end_send, end_recv,
):
    me = lax.axis_index("member")
    cluster = lax.axis_index("cluster")
    following = lax.rem(cluster + 1, CLUSTERS)
    preceding = lax.rem(cluster + CLUSTERS - 1, CLUSTERS)

    def panel_copy(s):
        return pltpu.make_async_copy(panels.at[s], rhs.at[s], panel_sem.at[s])

    def factor_copy(s, i):
        rows, cols = pl.ds(i * STEP, STEP), pl.ds(0, (i + 1) * STEP)
        return pltpu.make_async_copy(
            factors.at[s, rows, cols], factor.at[s, rows, cols], factor_sem.at[s, i]
        )

    for s in range(SUBS):
        for i in range(STEPS):
            factor_copy(s, i).start()
        panel_copy(s).start()

    barrier = pltpu.get_barrier_semaphore()

    @pl.loop(1, MEMBERS)
    def _(o):
        to = lax.rem(me + o, MEMBERS)
        pl.semaphore_signal(barrier, inc=1, device_id=(cluster, to), device_id_type=MESH)

    for other in (following, preceding):
        pl.semaphore_signal(barrier, inc=1, device_id=(other, me), device_id_type=MESH)

    row16, col16 = iota((16, PANEL), 0), iota((16, PANEL), 1)
    probe = jnp.where(row16 == 0, 1, jnp.where(row16 == 1, col16, 0)).astype(F32).astype(BF16)
    up_row, up_col = iota((LANES, LANES), 0), iota((LANES, LANES), 1)
    earlier = jnp.where((up_row // SHARE == up_col // SHARE) & (up_row < up_col), 1.0, 0.0)
    earlier = earlier.astype(BF16)
    for s in range(SUBS):
        glued = glue[s : s + 1, :]
        hot = jnp.where(iota((NDUAL, PANEL), 0) == glued, 1.0, 0.0).astype(BF16)
        found = dot(probe, hot, ((1,), (1,)))
        tiles = jnp.concatenate(
            [found[:, t * LANES : (t + 1) * LANES] for t in range(TILES)], axis=0
        )
        counts = dot(tiles.astype(BF16), earlier)
        for t in range(TILES):
            there = tiles[16 * t : 16 * t + 1] > 0.5
            where_from = tiles[16 * t + 1 : 16 * t + 2].astype(I32)
            columns[me * SUBS + s, t : t + 1, :] = jnp.where(there, where_from, PANEL)
            rank_rows[t, s : s + 1, :] = jnp.where(
                there, counts[16 * t : 16 * t + 1].astype(I32), -1
            )
        wide = jnp.concatenate([counts[16 * t : 16 * t + 16] for t in range(TILES)], axis=1)
        rank = dot(wide.astype(BF16), hot)[0:1].astype(I32)
        target = (glued // SHARE) * CAP + rank
        picks = jnp.where(iota((MEMBERS * CAP, PANEL), 0) == target, 1.0, 0.0)
        dispatch[s] = picks.astype(BF16)

    pl.semaphore_wait(barrier, MEMBERS + 1)

    def to_member(src, dst, send, recv, to):
        return pltpu.make_async_remote_copy(
            src_ref=src, dst_ref=dst, send_sem=send, recv_sem=recv,
            device_id=(cluster, to), device_id_type=MESH,
        )

    mine = pl.ds(me * SUBS, SUBS)

    @pl.loop(1, MEMBERS)
    def _(o):
        to = lax.rem(me + o, MEMBERS)
        to_member(columns.at[mine], columns.at[mine], column_send, column_recv.at[me], to).start()
        to_member(
            rank_rows.at[to // (LANES // SHARE)], ranks.at[me], rank_send, rank_recv.at[me], to
        ).start()
        to_member(loads, all_loads.at[me], load_send, load_recv.at[me], to).start()

    def solve(s):
        live = sizes[s]
        for i in range(STEPS):
            factor_copy(s, i).wait()
        for i in range(STEPS):
            rows = pl.ds(i * STEP, STEP)
            square = factor[s, rows, rows]
            row_id = iota(square.shape, 0)
            col_id = iota(square.shape, 1)
            keep = (col_id <= row_id) & (row_id + i * STEP < live)
            square = jnp.where(keep, square, jnp.where(row_id == col_id, 1.0, 0.0))
            high, low = split(block_inverse(square))
            diag_high[i] = high
            diag_low[i] = low
        panel_copy(s).wait()
        for i in range(STEPS):
            rows = pl.ds(i * STEP, STEP)
            part = rhs[s, rows, :]
            part = jnp.where(iota(part.shape, 0) + i * STEP < live, part, 0.0)
            found = split(dot3((diag_high[i], diag_low[i]), split(part)))
            solved_high[rows, :], solved_low[rows, :] = found
            if i < STEPS - 1:
                rest = pl.ds((i + 1) * STEP, ORDER - (i + 1) * STEP)
                rhs[s, rest, :] = rhs[s, rest, :] - dot3(split(factor[s, rest, rows]), found)
        high = solved_high[...]
        cross = dot(high, solved_low[...], ((0,), (0,)))
        local = dot(high, high, ((0,), (0,))) + (cross + cross.T)
        local_high, local_low = split(local)
        picks = dispatch[s]
        values = dot(picks, local_high) + dot(picks, local_low)
        outgoing[s] = values.reshape(MEMBERS, CAP, PANEL)
        incoming[s, me] = outgoing[s, me]

    @pl.loop(0, SUBS)
    def _(s):
        solve(s)

        @pl.loop(1, MEMBERS)
        def _(o):
            to = lax.rem(me + o, MEMBERS)
            to_member(
                outgoing.at[s, to], incoming.at[s, me], value_send.at[s], value_recv.at[s, me], to
            ).start()

    all_loads[me] = loads[...]
    ranks[me] = rank_rows[me // (LANES // SHARE)]

    @pl.loop(1, MEMBERS)
    def _(o):
        source = lax.rem(me - o + MEMBERS, MEMBERS)
        theirs = pl.ds(source * SUBS, SUBS)
        to_member(columns.at[theirs], columns.at[theirs], column_send, column_recv.at[source], source).wait_recv()
        to_member(rank_rows.at[0], ranks.at[source], rank_send, rank_recv.at[source], source).wait_recv()
        to_member(loads, all_loads.at[source], load_send, load_recv.at[source], source).wait_recv()

    slot = iota((CAP, LANES), 0)
    for s in range(SUBS):

        @pl.loop(0, MEMBERS)
        def _(o):
            source = lax.rem(me - o + MEMBERS, MEMBERS)

            @pl.when(o > 0)
            def _():
                to_member(
                    outgoing.at[s, 0], incoming.at[s, source], value_send.at[s],
                    value_recv.at[s, source], source,
                ).wait_recv()

            rows = pl.ds(pl.multiple_of((s * MEMBERS + o) * CAP, CAP), CAP)
            left = incoming[s, source, :, 0:LANES]
            right = incoming[s, source, :, LANES : 2 * LANES]
            for t in range(TILES):
                index = jnp.broadcast_to(columns[source * SUBS + s, t : t + 1, :], (CAP, LANES))
                lane = index & (LANES - 1)
                value = jnp.where(index < LANES, lanes_from(left, lane), lanes_from(right, lane))
                value = jnp.where(index < PANEL, value, 0.0)
                high, low = split(value)
                spread_high[rows, t * LANES : (t + 1) * LANES] = high
                spread_low[rows, t * LANES : (t + 1) * LANES] = low
            here = jnp.where(slot == ranks[source, s : s + 1, :], 1.0, 0.0)
            placing[rows, :] = here.astype(BF16)

    place = placing[...]
    stacked[...] = dot(place, spread_high[...], ((0,), (0,))) + dot(
        place, spread_low[...], ((0,), (0,))
    )
    owned = stacked[pl.ds(pl.multiple_of(lax.rem(me, LANES // SHARE) * SHARE, SHARE), SHARE), :]
    all_high, all_low = split(all_loads[...].reshape(NDUAL, PANEL))
    owned_high, owned_low = split(owned)
    product = dot(owned_high, all_high) + dot(owned_low, all_high) + dot(owned_high, all_low)
    raw[...] = product
    dual_out[...] = owned

    def end_copy(src, dst, k, to):
        return pltpu.make_async_remote_copy(
            src_ref=src, dst_ref=dst, send_sem=end_send.at[k], recv_sem=end_recv.at[k],
            device_id=(to, me), device_id_type=MESH,
        )

    up = end_copy(raw.at[pl.ds(SHARE - IFACE, IFACE)], before, 0, following)
    down = end_copy(raw.at[pl.ds(0, IFACE)], after, 1, preceding)
    up.start()
    down.start()
    products_out[pl.ds(IFACE, SHARE - 2 * IFACE), :] = product[IFACE : SHARE - IFACE]
    up.wait()
    down.wait()
    products_out[pl.ds(0, IFACE), :] = product[0:IFACE] + before[...]
    products_out[pl.ds(SHARE - IFACE, IFACE), :] = product[SHARE - IFACE :] + after[...]

    others = pl.ds(0, MEMBERS - 1)
    for s in range(SUBS):
        pltpu.make_async_copy(outgoing.at[s, others], incoming.at[s, others], value_send.at[s]).wait()
    pltpu.make_async_copy(
        columns.at[pl.ds(0, SUBS * (MEMBERS - 1))], columns.at[pl.ds(0, SUBS * (MEMBERS - 1))], column_send
    ).wait()
    pltpu.make_async_copy(ranks.at[others], ranks.at[others], rank_send).wait()
    pltpu.make_async_copy(all_loads.at[others], all_loads.at[others], load_send).wait()


def on_device(factors, panels, sizes, glue_index, loads):
    vmem = pl.BlockSpec(memory_space=pltpu.VMEM)
    dma = pltpu.SemaphoreType.DMA
    return pl.pallas_call(
        kernel,
        out_shape=(
            jax.ShapeDtypeStruct((SHARE, NDUAL), F32),
            jax.ShapeDtypeStruct((SHARE, PANEL), F32),
        ),
        in_specs=[
            pl.BlockSpec(memory_space=pltpu.SMEM),
            pl.BlockSpec(memory_space=pl.ANY),
            pl.BlockSpec(memory_space=pl.ANY),
            vmem,
            vmem,
        ],
        out_specs=(vmem, vmem),
        scratch_shapes=[
            pltpu.VMEM((SUBS, ORDER, ORDER), F32),
            pltpu.VMEM((SUBS, ORDER, PANEL), F32),
            pltpu.VMEM((ORDER, PANEL), BF16),
            pltpu.VMEM((ORDER, PANEL), BF16),
            pltpu.VMEM((STEPS, STEP, STEP), BF16),
            pltpu.VMEM((STEPS, STEP, STEP), BF16),
            pltpu.VMEM((SUBS, MEMBERS * CAP, PANEL), BF16),
            pltpu.VMEM((SUBS, MEMBERS, CAP, PANEL), F32),
            pltpu.VMEM((SUBS, MEMBERS, CAP, PANEL), F32),
            pltpu.VMEM((MEMBERS * SUBS, TILES, LANES), I32),
            pltpu.VMEM((TILES, SUBS, LANES), I32),
            pltpu.VMEM((MEMBERS, SUBS, LANES), I32),
            pltpu.VMEM((MEMBERS, SHARE, PANEL), F32),
            pltpu.VMEM((SUBS * MEMBERS * CAP, NDUAL), BF16),
            pltpu.VMEM((SUBS * MEMBERS * CAP, NDUAL), BF16),
            pltpu.VMEM((SUBS * MEMBERS * CAP, LANES), BF16),
            pltpu.VMEM((LANES, NDUAL), F32),
            pltpu.VMEM((SHARE, PANEL), F32),
            pltpu.VMEM((IFACE, PANEL), F32),
            pltpu.VMEM((IFACE, PANEL), F32),
            dma((SUBS, STEPS)),
            dma((SUBS,)),
            dma((SUBS,)),
            dma((SUBS, MEMBERS)),
            dma,
            dma((MEMBERS,)),
            dma,
            dma((MEMBERS,)),
            dma,
            dma((MEMBERS,)),
            dma((2,)),
            dma((2,)),
        ],
        compiler_params=pltpu.CompilerParams(
            collective_id=0, has_side_effects=True, vmem_limit_bytes=56 * 2**20
        ),
        name="dual_operator",
    )(sizes, factors, panels, glue_index, loads)


def solution(mesh):
    whole = ("cluster", "member")
    return jax.shard_map(
        on_device,
        mesh=mesh,
        in_specs=(P(whole, None, None), P(whole, None, None), P(whole), P(whole, None), P(whole, None)),
        out_specs=(P(whole, None), P(whole, None)),
        check_vma=False,
    )
```

time: 342 us -> 55 us (0.16); the launches traced: 338 us -> 54.7 us
  other arithmetic: 168 us -> 0 us
  matrix products: 66.6 us -> 0 us
  starting transfers between devices: 65.4 us -> 0 us
  Pallas kernels: 0 us -> 51.1 us
  waiting for transfers between devices: 17.8 us -> 0 us
  local copies, waits for them, and re-layouts: 15.8 us -> 2.94 us
    another operation x26 -> x0, other arithmetic: 128 us -> none  [advance(): lax.linalg.triangular_solve(square, remainder, left_side=True, lower=True)]
    dot_general x146 -> x0, matrix products: 62.5 us -> none  [the longest x64 32 us: place_source(): jnp.dot(block_values, column_map, precision=PRECISE, preferred_element_ty...]
    all_to_all x3 -> x0, starting transfers between devices: 62.1 us -> none  [the longest x1 49.5 us: on_device(): lax.all_to_all(sent_values, 'member', split_axis=0, concat_axis=0, tiled=...]
    pallas_call x0 -> x1, Pallas kernels: none -> 51.1 us  [on_device(): pl.pallas_call(kernel, out_shape=(jax.ShapeDtypeStruct((SHARE, NDUAL), F3...]
    select_n x21 -> x0, other arithmetic: 20.1 us -> none  [the longest x13 16.3 us: live_lower(): jnp.where(keeping, full_rows, (row_ids == col_ids).astype(jnp.float32))]
    lt x27 -> x0, other arithmetic: 16.9 us -> none  [the longest x13 7.86 us: live_lower(): row_ids < live_size]
    all_to_all x3 -> x0, waiting for transfers between devices: 16.9 us -> none  [the longest x1 16.9 us: on_device(): lax.all_to_all(sent_values, 'member', split_axis=0, concat_axis=0, tiled=...]
    squeeze x1 -> x0, local copies, waits for them, and re-layouts: 8.49 us -> none  [on_device(): solved = solve_panel(factors[sub_slot], panels[sub_slot], sizes[sub_slot])]
  transfers between devices with their start and end apart: 5 -> 0, of which waited for: 2 -> 0; matrix products, arithmetic and copies ran while one was open for 72% -> 0% of each run, Pallas kernels for 0% -> 0%
where the time goes in v1:
time: 55 us; the launch traced here: 54.7 us
  Pallas kernels  51.1 us (93%)
  local copies, waits for them, and re-layouts  2.94 us (5%)
  between operations  0.64 us (1%)
    pallas_call x1, Pallas kernels, on_device(): pl.pallas_call(kernel, out_shape=(jax.ShapeDtypeStruct((SHARE, NDUAL), F3...  51.1 us
    unnamed x2, local copies, waits for them, and re-layouts  2.94 us

profile of v1, /device:TPU:1, one launch (start us, length us, event | category | flops | bytes accessed | tf_op | source)
XLA Modules:
  0.0 54.7 jit_solution(13974207031088080279)
XLA Ops:
  0.6 51.1 %dual_operator.1 = (f32[32,1024]{1,0:T(8,128)}, f32[32,256]{1,0:T(8,128)}) custom-call(s32[2]{0:T(128)} %sizes.1, f32[2,1024,1024]{2,1,0:T(8,128)} %factors.1, f32[2,1024,256]{2,1,0:T(8,128)} %panels.1, s32[2,256]{1,0:T(2,128)} %glue.1, f32[32,256]{1,0:T(8,128)} %loads.1), custom_call_target="tpu_custom_call" | custom-call | tf_op jit(solution)/shard_map/dual_operator/pallas_call | solution.py:307
  51.8 1.6 %copy.9 = f32[32,1024]{1,0:T(8,128)} copy(f32[32,1024]{1,0:T(8,128)} %get-tuple-element.4) | data formatting | bytes 262144
  53.4 1.4 %copy.10 = f32[32,256]{1,0:T(8,128)} copy(f32[32,256]{1,0:T(8,128)} %get-tuple-element.5) | data formatting | bytes 65536

commit v2 on v1

v2 whole, which is shorter than its diff:
```python
import functools

import jax
import jax.numpy as jnp
from jax import lax
from jax.experimental import pallas as pl
from jax.experimental.pallas import tpu as pltpu
from jax.sharding import PartitionSpec as P

ORDER = 1024
PANEL = 256
NDUAL = 1024
MEMBERS = 32
CLUSTERS = 8
CORES = 2
CHIPS = MEMBERS // CORES
SIDE = 4
AROUND = [(dx, dy) for dy in (1, 3, 2, 0) for dx in (1, 3, 0, 2) if (dx, dy) != (0, 0)]
GROUP = 8
SHARE = NDUAL // MEMBERS
CAP = 2 * PANEL // MEMBERS
SUBS = 2
IFACE = 8
LANES = 128
STEP = 128
STEPS = ORDER // STEP
BATCH = 4
FOLD = 4
BASE = 32
TILES = NDUAL // LANES
F32, BF16, I32 = jnp.float32, jnp.bfloat16, jnp.int32
MESH = pl.DeviceIdType.MESH


def iota(shape, dim):
    return lax.broadcasted_iota(I32, shape, dim)


def split(x):
    high = x.astype(BF16)
    return high, (x - high.astype(F32)).astype(BF16)


def dot(a, b, dims=((1,), (0,))):
    return lax.dot_general(a, b, (dims, ((), ())), preferred_element_type=F32)


def dot3(a, b):
    a_high, a_low = a
    b_high, b_low = b
    left = jnp.concatenate([a_high, a_low], axis=1)
    right = jnp.concatenate([b_high, b_high], axis=0)
    return dot(left, right) + dot(a_high, b_low)


def lanes_from(x, index):
    numbers = lax.GatherDimensionNumbers(
        offset_dims=(),
        collapsed_slice_dims=(1,),
        start_index_map=(1,),
        operand_batching_dims=(0,),
        start_indices_batching_dims=(0,),
    )
    return lax.gather(
        x, index[..., None], numbers, (1, 1), mode=lax.GatherScatterMode.PROMISE_IN_BOUNDS
    )


def base_inverses(blocks):
    count = BASE // 8
    group = iota((BASE, LANES), 1) // BASE
    lane = iota((8, LANES), 1)
    first, within = (lane // BASE) * BASE, lane % BASE
    row_ids = [iota((8, LANES), 0) + v * 8 for v in range(count)]
    units, results, scales = [], [], []
    for block in blocks:
        packed = jnp.zeros((BASE, LANES), F32)
        for q in range(LANES // BASE):
            packed = jnp.where(group == q, block[q * BASE : (q + 1) * BASE], packed)
        unit, scale = [], jnp.zeros((1, LANES), F32)
        for v in range(count):
            rows = packed[v * 8 : (v + 1) * 8]
            inverse = 1.0 / lanes_from(rows, first + row_ids[v])
            unit.append(jnp.where(within < row_ids[v], rows * inverse, 0.0))
            own = jnp.where(within == row_ids[v], inverse, 0.0)
            scale = scale + jnp.sum(own, axis=0, keepdims=True)
        units.append(unit)
        scales.append(scale)
        results.append([jnp.where(within == row_ids[v], 1.0, 0.0) for v in range(count)])
    for j in range(BASE - 1):
        for unit, result in zip(units, results):
            row = jnp.broadcast_to(result[j // 8][j % 8 : j % 8 + 1], (8, LANES))
            for v in range((j + 1) // 8, count):
                result[v] = result[v] - lanes_from(unit[v], first + j) * row
    inverses = []
    for result, scale in zip(results, scales):
        scaled = jnp.concatenate(result, axis=0) * scale
        inverses.append(
            jnp.concatenate(
                [jnp.where(group == q, scaled, 0.0) for q in range(LANES // BASE)], axis=0
            )
        )
    return inverses


def doubled(inverses, blocks, size):
    row, col = iota((STEP, STEP), 0) // size, iota((STEP, STEP), 1) // size
    below = (row % 2 == 1) & (col == row - 1)
    odd = range(1, STEP // size, 2)
    halves = [split(inverse) for inverse in inverses]
    firsts = []
    for (high, low), block in zip(halves, blocks):
        lower = [
            jnp.concatenate([part[k * size : (k + 1) * size] for k in odd], axis=0)
            for part in (high, low)
        ]
        firsts.append(dot3(lower, split(jnp.where(below, block, 0.0))))
    results = []
    for inverse, half, part in zip(inverses, halves, firsts):
        change = dot3(split(part), half)
        pieces = []
        for k in range(STEP // size):
            piece = inverse[k * size : (k + 1) * size]
            if k % 2:
                piece = piece - change[(k // 2) * size : (k // 2 + 1) * size]
            pieces.append(piece)
        results.append(jnp.concatenate(pieces, axis=0))
    return results


def kernel(
    sizes, factors, panels, glue, loads, dual_out, products_out,
    factor, rhs, solved_high, solved_low, step_high, step_low, dispatch,
    outgoing, incoming, columns, own_tile, ranks, all_loads, inverted,
    spread_high, spread_low, placing, stacked, raw, before, after,
    factor_sem, panel_sem, value_send, value_recv, column_send, column_recv,
    load_send, load_recv, pair_send, pair_recv, end_send, end_recv,
):
    me = lax.axis_index("member")
    cluster = lax.axis_index("cluster")
    chip, core = me // CORES, lax.rem(me, CORES)
    partner = chip * CORES + (1 - core)
    following = lax.rem(cluster + 1, CLUSTERS)
    preceding = lax.rem(cluster + CLUSTERS - 1, CLUSTERS)

    def panel_copy(s):
        return pltpu.make_async_copy(panels.at[s], rhs.at[s], panel_sem.at[s])

    def factor_copy(s, i):
        rows, cols = pl.ds(i * STEP, STEP), pl.ds(0, (i + 1) * STEP)
        return pltpu.make_async_copy(
            factors.at[s, rows, cols], factor.at[s, rows, cols], factor_sem.at[s, i]
        )

    for s in range(SUBS):
        for i in range(STEPS):
            factor_copy(s, i).start()
        panel_copy(s).start()

    barrier = pltpu.get_barrier_semaphore()

    @pl.loop(1, MEMBERS)
    def _(o):
        to = lax.rem(me + o, MEMBERS)
        pl.semaphore_signal(barrier, inc=1, device_id=(cluster, to), device_id_type=MESH)

    for other in (following, preceding):
        pl.semaphore_signal(barrier, inc=1, device_id=(other, me), device_id_type=MESH)

    row16, col16 = iota((16, PANEL), 0), iota((16, PANEL), 1)
    probe = jnp.where(row16 == 0, 1, jnp.where(row16 == 1, col16, 0)).astype(F32).astype(BF16)
    up_row, up_col = iota((LANES, LANES), 0), iota((LANES, LANES), 1)
    earlier = jnp.where((up_row // SHARE == up_col // SHARE) & (up_row < up_col), 1.0, 0.0)
    earlier = earlier.astype(BF16)
    for s in range(SUBS):
        glued = glue[s : s + 1, :]
        hot = jnp.where(iota((NDUAL, PANEL), 0) == glued, 1.0, 0.0).astype(BF16)
        found = dot(probe, hot, ((1,), (1,)))
        tiles = jnp.concatenate(
            [found[:, t * LANES : (t + 1) * LANES] for t in range(TILES)], axis=0
        )
        counts = dot(tiles.astype(BF16), earlier)
        for t in range(TILES):
            there = tiles[16 * t : 16 * t + 1] > 0.5
            where_from = tiles[16 * t + 1 : 16 * t + 2].astype(I32)
            columns[chip, core, s, t : t + 1, :] = jnp.where(there, where_from, PANEL)
        wide = jnp.concatenate([counts[16 * t : 16 * t + 16] for t in range(TILES)], axis=1)
        rank = dot(wide.astype(BF16), hot)[0:1].astype(I32)
        target = (glued // SHARE) * CAP + rank
        picks = jnp.where(iota((MEMBERS * CAP, PANEL), 0) == target, 1.0, 0.0)
        dispatch[s] = picks.astype(BF16)

    def to_member(src, dst, send, recv, to):
        return pltpu.make_async_remote_copy(
            src_ref=src, dst_ref=dst, send_sem=send, recv_sem=recv,
            device_id=(cluster, to), device_id_type=MESH,
        )

    def chip_at(dx, dy):
        y, x = chip // SIDE, lax.rem(chip, SIDE)
        return lax.rem(y + dy, SIDE) * SIDE + lax.rem(x + dx, SIDE)

    def squares(s):
        live = sizes[s]
        found = []
        for i in range(STEPS):
            rows = pl.ds(i * STEP, STEP)
            square = factor[s, rows, rows]
            row_id, col_id = iota(square.shape, 0), iota(square.shape, 1)
            keep = (col_id <= row_id) & (row_id + i * STEP < live)
            found.append(jnp.where(keep, square, jnp.where(row_id == col_id, 1.0, 0.0)))
        return found

    def invert(s):
        for i in range(STEPS):
            factor_copy(s, i).wait()
        blocks = squares(s)
        for k in range(0, STEPS, BATCH):
            for i, found in enumerate(base_inverses(blocks[k : k + BATCH])):
                inverted[k + i] = found
        found = [inverted[i] for i in range(STEPS)]
        size = BASE
        while size < STEP:
            found = doubled(found, blocks, size)
            size *= 2
        for i in range(STEPS):
            half = split(found[i])
            step_high[s, i, 0:STEP], step_low[s, i, 0:STEP] = half
            if i < STEPS - 1:
                under = factor[s, pl.ds((i + 1) * STEP, STEP), pl.ds(i * STEP, STEP)]
                onward = split(dot3(split(under), half))
                step_high[s, i, STEP : 2 * STEP], step_low[s, i, STEP : 2 * STEP] = onward

    with jax.named_scope("invert"):
        invert(0)

    with jax.named_scope("barrier"):
        pl.semaphore_wait(barrier, MEMBERS + 1)

    def chip_at(dx, dy):
        y, x = chip // SIDE, lax.rem(chip, SIDE)
        return lax.rem(y + dy, SIDE) * SIDE + lax.rem(x + dx, SIDE)

    def along(first, second):
        return chip_at(
            first * (1 - core) + second * core, first * core + second * (1 - core)
        )

    def column_copy(origin, to):
        return to_member(
            columns.at[origin, core], columns.at[origin, core], column_send,
            column_recv.at[origin], to * CORES + core,
        )

    def load_copy(source, origin, to):
        return to_member(
            source, all_loads.at[origin, core], load_send, load_recv.at[origin], to * CORES + core
        )

    every = pl.ds(0, CHIPS)

    def pair_copy(ref, which, k):
        return to_member(
            ref.at[every, which], ref.at[every, which], pair_send.at[k], pair_recv.at[k], partner
        )

    with jax.named_scope("share"):
        for dx, dy in AROUND:
            column_copy(chip, chip_at(dx, dy)).start()
        for k in (1, 3, 2):
            load_copy(loads, chip, along(k, 0)).start()
            load_copy(loads, chip, along(0, k)).start()
        all_loads[chip, core] = loads[...]

    def substitute(s):
        live = sizes[s]
        panel_copy(s).wait()

        def masked(i, part):
            return jnp.where(iota(part.shape, 0) + i * STEP < live, part, 0.0)

        part = masked(0, rhs[s, 0:STEP, :])
        squared, cross = [], []
        for i in range(STEPS):
            halves = split(part)
            tall = STEP if i == STEPS - 1 else 2 * STEP
            both = dot3((step_high[s, i, 0:tall], step_low[s, i, 0:tall]), halves)
            if i < STEPS - 1:
                part = masked(i + 1, rhs[s, (i + 1) * STEP : (i + 2) * STEP, :] - both[STEP:])
            found = split(both[0:STEP])
            solved_high[i * STEP : (i + 1) * STEP], solved_low[i * STEP : (i + 1) * STEP] = found
            if i < STEPS - 2:
                rest = pl.ds((i + 2) * STEP, ORDER - (i + 2) * STEP)
                left = split(factor[s, rest, pl.ds(i * STEP, STEP)])
                rhs[s, rest, :] = rhs[s, rest, :] - dot3(left, found)
            if i % FOLD == FOLD - 1:
                done = pl.ds((i + 1 - FOLD) * STEP, FOLD * STEP)
                high = solved_high[done, :]
                squared.append(dot(high, high, ((0,), (0,))))
                cross.append(dot(high, solved_low[done, :], ((0,), (0,))))
        crossed = sum(cross[1:], cross[0])
        local = sum(squared[1:], squared[0]) + (crossed + crossed.T)
        local_high, local_low = split(local)
        picks = dispatch[s]
        values = dot(picks, local_high) + dot(picks, local_low)
        outgoing[s] = values.reshape(MEMBERS, CAP, PANEL)
        incoming[s, me] = outgoing[s, me]

    for s in range(SUBS):
        if s:
            with jax.named_scope("invert"):
                invert(1)

            with jax.named_scope("forward"):
                for first in (3, 1, 2):
                    origin = along(first, 0)
                    load_copy(loads, origin, origin).wait_recv()
                    for k in (1, 3, 2):
                        load_copy(all_loads.at[origin, core], origin, along(0, k)).start()
                for dx, dy in AROUND:
                    origin = chip_at(dx, dy)
                    column_copy(origin, origin).wait_recv()
                pair_copy(columns, core, 0).start()

        with jax.named_scope("substitute"):
            substitute(s)

        def send(to):
            to_member(
                outgoing.at[s, to], incoming.at[s, me], value_send.at[s], value_recv.at[s, me], to
            ).start()

        with jax.named_scope("send"):

            @pl.loop(0, CORES)
            def _(dc):
                for dx, dy in AROUND:
                    send(chip_at(dx, dy) * CORES + lax.rem(core + dc, CORES))

            send(partner)

    with jax.named_scope("pair"):
        pair_copy(columns, 1 - core, 0).wait_recv()

    with jax.named_scope("ranks"):
        @pl.loop(0, MEMBERS)
        def _(m):
            for s in range(SUBS):
                tile = columns[m // CORES, lax.rem(m, CORES), s, pl.ds(me // (LANES // SHARE), 1), :]
                own_tile[pl.ds(s * MEMBERS + m, 1), :] = tile

        shift = lax.rem(me, LANES // SHARE) * SHARE
        own = own_tile[...]
        lane = iota(own.shape, 1)
        own = lanes_from(own, lax.rem(lane + shift, LANES))
        there = (own < PANEL) & (lane < SHARE)
        order = dot(jnp.where(there, 1.0, 0.0).astype(BF16), earlier).astype(I32)
        ranks[...] = jnp.where(there, order, -1)

    slot = iota((CAP, LANES), 0)
    stacked[...] = jnp.zeros_like(stacked)

    def place_one(s, source, k):
        rows = slice(k * CAP, (k + 1) * CAP)
        left = incoming[s, source, :, 0:LANES]
        right = incoming[s, source, :, LANES : 2 * LANES]
        source_chip, source_core = source // CORES, lax.rem(source, CORES)
        for t in range(TILES):
            index = jnp.broadcast_to(columns[source_chip, source_core, s, t : t + 1, :], (CAP, LANES))
            lane = index & (LANES - 1)
            value = jnp.where(index < LANES, lanes_from(left, lane), lanes_from(right, lane))
            value = jnp.where(index < PANEL, value, 0.0)
            high, low = split(value)
            spread_high[rows, t * LANES : (t + 1) * LANES] = high
            spread_low[rows, t * LANES : (t + 1) * LANES] = low
        here = jnp.where(slot == ranks[pl.ds(s * MEMBERS + source, 1), :], 1.0, 0.0)
        placing[rows, :] = here.astype(BF16)

    for s in range(SUBS):
        with jax.named_scope("place"):

            @pl.loop(0, CORES)
            def _(dc):
                if s:

                    @pl.when(dc == CORES - 1)
                    def _():
                        for second in (1, 3, 2):
                            for first in range(SIDE):
                                origin = along(first, second)
                                load_copy(loads, origin, origin).wait_recv()
                        pair_copy(all_loads, core, 1).start()

                for half in range(CHIPS // GROUP):
                    sources = [
                        chip_at((SIDE - dx) % SIDE, (SIDE - dy) % SIDE) * CORES
                        + lax.rem(core + dc, CORES)
                        for dx, dy in (AROUND + [(0, 0)])[half * GROUP : (half + 1) * GROUP]
                    ]

                    def wait(source):
                        to_member(
                            outgoing.at[s, 0], incoming.at[s, source], value_send.at[s],
                            value_recv.at[s, source], source,
                        ).wait_recv()

                    last = half == CHIPS // GROUP - 1
                    for source in sources[:-1] if last else sources:
                        wait(source)
                    if last:
                        pl.when(dc > 0)(functools.partial(wait, partner))
                    for k, source in enumerate(sources):
                        place_one(s, source, k)
                    place = placing[...]
                    part = dot(place, spread_high[...], ((0,), (0,))) + dot(
                        place, spread_low[...], ((0,), (0,))
                    )
                    part = part[0:SHARE]
                    stacked[...] = stacked[...] + part

    with jax.named_scope("apply"):
        pair_copy(all_loads, 1 - core, 1).wait_recv()
        owned = stacked[...]
        all_high, all_low = split(all_loads[...].reshape(NDUAL, PANEL))
        owned_high, owned_low = split(owned)
        product = dot(owned_high, all_high) + dot(owned_low, all_high) + dot(owned_high, all_low)
        raw[...] = product
        dual_out[...] = owned

    def end_copy(src, dst, k, to):
        return pltpu.make_async_remote_copy(
            src_ref=src, dst_ref=dst, send_sem=end_send.at[k], recv_sem=end_recv.at[k],
            device_id=(to, me), device_id_type=MESH,
        )

    up = end_copy(raw.at[pl.ds(SHARE - IFACE, IFACE)], before, 0, following)
    down = end_copy(raw.at[pl.ds(0, IFACE)], after, 1, preceding)
    with jax.named_scope("ends"):
        up.start()
        down.start()
        products_out[pl.ds(IFACE, SHARE - 2 * IFACE), :] = product[IFACE : SHARE - IFACE]
        up.wait()
        down.wait()
        products_out[pl.ds(0, IFACE), :] = product[0:IFACE] + before[...]
        products_out[pl.ds(SHARE - IFACE, IFACE), :] = product[SHARE - IFACE :] + after[...]

    others = pl.ds(0, MEMBERS - 1)
    with jax.named_scope("drain"):
        for s in range(SUBS):
            pltpu.make_async_copy(outgoing.at[s, others], incoming.at[s, others], value_send.at[s]).wait()
        far = pl.ds(0, CHIPS - 1)
        pltpu.make_async_copy(columns.at[far, 0], columns.at[far, 0], column_send).wait()
        pltpu.make_async_copy(all_loads.at[far, 0], all_loads.at[far, 0], load_send).wait()
        pair_copy(columns, core, 0).wait_send()
        pair_copy(all_loads, core, 1).wait_send()


def hand_over(owned, products, owned_out, products_out):
    owned_out[...] = owned[...]
    products_out[...] = products[...]


def on_device(factors, panels, sizes, glue_index, loads):
    vmem = pl.BlockSpec(memory_space=pltpu.VMEM)
    dma = pltpu.SemaphoreType.DMA
    owned, products = pl.pallas_call(
        kernel,
        out_shape=(
            jax.ShapeDtypeStruct((SHARE, NDUAL), F32),
            jax.ShapeDtypeStruct((SHARE, PANEL), F32),
        ),
        in_specs=[
            pl.BlockSpec(memory_space=pltpu.SMEM),
            pl.BlockSpec(memory_space=pl.ANY),
            pl.BlockSpec(memory_space=pl.ANY),
            vmem,
            vmem,
        ],
        out_specs=(vmem, vmem),
        scratch_shapes=[
            pltpu.VMEM((SUBS, ORDER, ORDER), F32),
            pltpu.VMEM((SUBS, ORDER, PANEL), F32),
            pltpu.VMEM((ORDER, PANEL), BF16),
            pltpu.VMEM((ORDER, PANEL), BF16),
            pltpu.VMEM((SUBS, STEPS, 2 * STEP, STEP), BF16),
            pltpu.VMEM((SUBS, STEPS, 2 * STEP, STEP), BF16),
            pltpu.VMEM((SUBS, MEMBERS * CAP, PANEL), BF16),
            pltpu.VMEM((SUBS, MEMBERS, CAP, PANEL), F32),
            pltpu.VMEM((SUBS, MEMBERS, CAP, PANEL), F32),
            pltpu.VMEM((CHIPS, CORES, SUBS, TILES, LANES), I32),
            pltpu.VMEM((SUBS * MEMBERS, LANES), I32),
            pltpu.VMEM((SUBS * MEMBERS, LANES), I32),
            pltpu.VMEM((CHIPS, CORES, SHARE, PANEL), F32),
            pltpu.VMEM((STEPS, STEP, STEP), F32),
            pltpu.VMEM((GROUP * CAP, NDUAL), BF16),
            pltpu.VMEM((GROUP * CAP, NDUAL), BF16),
            pltpu.VMEM((GROUP * CAP, LANES), BF16),
            pltpu.VMEM((SHARE, NDUAL), F32),
            pltpu.VMEM((SHARE, PANEL), F32),
            pltpu.VMEM((IFACE, PANEL), F32),
            pltpu.VMEM((IFACE, PANEL), F32),
            dma((SUBS, STEPS)),
            dma((SUBS,)),
            dma((SUBS,)),
            dma((SUBS, MEMBERS)),
            dma,
            dma((CHIPS,)),
            dma,
            dma((CHIPS,)),
            dma((2,)),
            dma((2,)),
            dma((2,)),
            dma((2,)),
        ],
        compiler_params=pltpu.CompilerParams(
            collective_id=0, has_side_effects=True, vmem_limit_bytes=56 * 2**20
        ),
        name="dual_operator",
    )(sizes, factors, panels, glue_index, loads)
    return pl.pallas_call(
        hand_over,
        out_shape=(
            jax.ShapeDtypeStruct((SHARE, NDUAL), F32),
            jax.ShapeDtypeStruct((SHARE, PANEL), F32),
        ),
        in_specs=[vmem, vmem],
        out_specs=(vmem, vmem),
        name="hand_over",
    )(owned, products)


def solution(mesh):
    whole = ("cluster", "member")
    return jax.shard_map(
        on_device,
        mesh=mesh,
        in_specs=(P(whole, None, None), P(whole, None, None), P(whole), P(whole, None), P(whole, None)),
        out_specs=(P(whole, None), P(whole, None)),
        check_vma=False,
    )
```

time: 55 us -> 39.9 us (0.73)
  Pallas kernels: 51.1 us -> 39.1 us
  local copies, waits for them, and re-layouts: 2.94 us -> 0 us
    pallas_call x1, Pallas kernels: 51.1 us -> 37.6 us  [on_device(): pl.pallas_call(kernel, out_shape=(jax.ShapeDtypeStruct((SHARE, NDUAL), F3...]
    unnamed x2 -> x0, local copies, waits for them, and re-layouts: 2.94 us -> none
    pallas_call x0 -> x1, Pallas kernels: none -> 1.57 us  [on_device(): pl.pallas_call(hand_over, out_shape=(jax.ShapeDtypeStruct((SHARE, NDUAL),...]
where the time goes in v2:
time: 39.9 us; the launch traced here: 39.8 us
  Pallas kernels  39.1 us (98%)
  between operations  0.64 us (2%)
    pallas_call x1, Pallas kernels, on_device(): pl.pallas_call(kernel, out_shape=(jax.ShapeDtypeStruct((SHARE, NDUAL), F3...  37.6 us
    pallas_call x1, Pallas kernels, on_device(): pl.pallas_call(hand_over, out_shape=(jax.ShapeDtypeStruct((SHARE, NDUAL),...  1.57 us

profile of v2, /device:TPU:1, one launch (start us, length us, event | category | flops | bytes accessed | tf_op | source)
XLA Modules:
  0.0 39.8 jit_solution(10132169356103079532)
XLA Ops:
  0.6 37.6 %dual_operator.1 = (f32[32,1024]{1,0:T(8,128)}, f32[32,256]{1,0:T(8,128)}) custom-call(s32[2]{0:T(128)} %sizes.1, f32[2,1024,1024]{2,1,0:T(8,128)} %factors.1, f32[2,1024,256]{2,1,0:T(8,128)} %panels.1, s32[2,256]{1,0:T(2,128)} %glue.1, f32[32,256]{1,0:T(8,128)} %loads.1), custom_call_target="tpu_custom_call" | custom-call | tf_op jit(solution)/shard_map/dual_operator/pallas_call | solution.py:466
  38.2 1.6 %hand_over.1 = (f32[32,1024]{1,0:T(8,128)}, f32[32,256]{1,0:T(8,128)}) custom-call(f32[32,1024]{1,0:T(8,128)} %get-tuple-element.4.owned, f32[32,256]{1,0:T(8,128)} %get-tuple-element.5.products), custom_call_target="tpu_custom_call" | custom-call | tf_op jit(solution)/shard_map/hand_over/pallas_call | solution.py:520

commit v3 on v2

--- a/solution.py
+++ b/solution.py
@@ -16,7 +16,7 @@
 CHIPS = MEMBERS // CORES
 SIDE = 4
 AROUND = [(dx, dy) for dy in (1, 3, 2, 0) for dx in (1, 3, 0, 2) if (dx, dy) != (0, 0)]
-GROUP = 8
+GROUP = 4
 SHARE = NDUAL // MEMBERS
 CAP = 2 * PANEL // MEMBERS
 SUBS = 2
@@ -130,7 +130,7 @@
 
 def kernel(
     sizes, factors, panels, glue, loads, dual_out, products_out,
-    factor, rhs, solved_high, solved_low, step_high, step_low, dispatch,
+    factor, rhs, solved_high, solved_low, step_high, step_low,
     outgoing, incoming, columns, own_tile, ranks, all_loads, inverted,
     spread_high, spread_low, placing, stacked, raw, before, after,
     factor_sem, panel_sem, value_send, value_recv, column_send, column_recv,
@@ -152,10 +152,12 @@
             factors.at[s, rows, cols], factor.at[s, rows, cols], factor_sem.at[s, i]
         )
 
-    for s in range(SUBS):
+    def start_copies(s):
         for i in range(STEPS):
             factor_copy(s, i).start()
         panel_copy(s).start()
+
+    start_copies(0)
 
     barrier = pltpu.get_barrier_semaphore()
 
@@ -172,6 +174,7 @@
     up_row, up_col = iota((LANES, LANES), 0), iota((LANES, LANES), 1)
     earlier = jnp.where((up_row // SHARE == up_col // SHARE) & (up_row < up_col), 1.0, 0.0)
     earlier = earlier.astype(BF16)
+    targets = []
     for s in range(SUBS):
         glued = glue[s : s + 1, :]
         hot = jnp.where(iota((NDUAL, PANEL), 0) == glued, 1.0, 0.0).astype(BF16)
@@ -187,8 +190,7 @@
         wide = jnp.concatenate([counts[16 * t : 16 * t + 16] for t in range(TILES)], axis=1)
         rank = dot(wide.astype(BF16), hot)[0:1].astype(I32)
         target = (glued // SHARE) * CAP + rank
-        picks = jnp.where(iota((MEMBERS * CAP, PANEL), 0) == target, 1.0, 0.0)
-        dispatch[s] = picks.astype(BF16)
+        targets.append(target)
 
     def to_member(src, dst, send, recv, to):
         return pltpu.make_async_remote_copy(
@@ -214,6 +216,8 @@
     def invert(s):
         for i in range(STEPS):
             factor_copy(s, i).wait()
+        if s + 1 < SUBS:
+            start_copies(s + 1)
         blocks = squares(s)
         for k in range(0, STEPS, BATCH):
             for i, found in enumerate(base_inverses(blocks[k : k + BATCH])):
@@ -265,11 +269,11 @@
         )
 
     with jax.named_scope("share"):
-        for dx, dy in AROUND:
-            column_copy(chip, chip_at(dx, dy)).start()
         for k in (1, 3, 2):
             load_copy(loads, chip, along(k, 0)).start()
             load_copy(loads, chip, along(0, k)).start()
+        for dx, dy in AROUND:
+            column_copy(chip, chip_at(dx, dy)).start()
         all_loads[chip, core] = loads[...]
 
     def substitute(s):
@@ -301,7 +305,7 @@
         crossed = sum(cross[1:], cross[0])
         local = sum(squared[1:], squared[0]) + (crossed + crossed.T)
         local_high, local_low = split(local)
-        picks = dispatch[s]
+        picks = jnp.where(iota((MEMBERS * CAP, PANEL), 0) == targets[s], 1.0, 0.0).astype(BF16)
         values = dot(picks, local_high) + dot(picks, local_low)
         outgoing[s] = values.reshape(MEMBERS, CAP, PANEL)
         incoming[s, me] = outgoing[s, me]
@@ -317,13 +321,16 @@
                     load_copy(loads, origin, origin).wait_recv()
                     for k in (1, 3, 2):
                         load_copy(all_loads.at[origin, core], origin, along(0, k)).start()
+
+        with jax.named_scope("substitute"):
+            substitute(s)
+
+        if s:
+            with jax.named_scope("gathered"):
                 for dx, dy in AROUND:
                     origin = chip_at(dx, dy)
                     column_copy(origin, origin).wait_recv()
                 pair_copy(columns, core, 0).start()
-
-        with jax.named_scope("substitute"):
-            substitute(s)
 
         def send(to):
             to_member(
@@ -484,7 +491,6 @@
             pltpu.VMEM((ORDER, PANEL), BF16),
             pltpu.VMEM((SUBS, STEPS, 2 * STEP, STEP), BF16),
             pltpu.VMEM((SUBS, STEPS, 2 * STEP, STEP), BF16),
-            pltpu.VMEM((SUBS, MEMBERS * CAP, PANEL), BF16),
             pltpu.VMEM((SUBS, MEMBERS, CAP, PANEL), F32),
             pltpu.VMEM((SUBS, MEMBERS, CAP, PANEL), F32),
             pltpu.VMEM((CHIPS, CORES, SUBS, TILES, LANES), I32),

time: 39.9 us -> 41 us (1.028)
  Pallas kernels: 39.1 us -> 40.1 us
    pallas_call x1, Pallas kernels: 37.6 us -> 38.6 us  [on_device(): pl.pallas_call(kernel, out_shape=(jax.ShapeDtypeStruct((SHARE, NDUAL), F3...]
where the time goes in v3:
time: 41 us; the launch traced here: 40.8 us
  Pallas kernels  40.1 us (98%)
  between operations  0.64 us (2%)
    pallas_call x1, Pallas kernels, on_device(): pl.pallas_call(kernel, out_shape=(jax.ShapeDtypeStruct((SHARE, NDUAL), F3...  38.6 us
    pallas_call x1, Pallas kernels, on_device(): pl.pallas_call(hand_over, out_shape=(jax.ShapeDtypeStruct((SHARE, NDUAL),...  1.57 us

profile of v3, /device:TPU:1, one launch (start us, length us, event | category | flops | bytes accessed | tf_op | source)
XLA Modules:
  0.0 40.8 jit_solution(4128713222872921426)
XLA Ops:
  0.6 38.6 %dual_operator.1 = (f32[32,1024]{1,0:T(8,128)}, f32[32,256]{1,0:T(8,128)}) custom-call(s32[2]{0:T(128)} %sizes.1, f32[2,1024,1024]{2,1,0:T(8,128)} %factors.1, f32[2,1024,256]{2,1,0:T(8,128)} %panels.1, s32[2,256]{1,0:T(2,128)} %glue.1, f32[32,256]{1,0:T(8,128)} %loads.1), custom_call_target="tpu_custom_call" | custom-call | tf_op jit(solution)/shard_map/dual_operator/pallas_call | solution.py:473
  39.2 1.6 %hand_over.1 = (f32[32,1024]{1,0:T(8,128)}, f32[32,256]{1,0:T(8,128)}) custom-call(f32[32,1024]{1,0:T(8,128)} %get-tuple-element.4.owned, f32[32,256]{1,0:T(8,128)} %get-tuple-element.5.products), custom_call_target="tpu_custom_call" | custom-call | tf_op jit(solution)/shard_map/hand_over/pallas_call | solution.py:526
